TPU v7x, 32 devices: a whole 2x2x4 slice. The times are simulated.
32 devices in a mesh: grp: 2 (over y), row: 16 (over z, x, core).
Axes of the slice: x: 2, y: 2, z: 4, core: 2. Of those that a mesh axis runs over, the one named last changes fastest.
Arguments:
- item_ids: int32 [128, 512], P(('grp', 'row')), may hold values from 0 to 49999, as said below
- lengths: int32 [128], P(('grp', 'row')), may hold values from 358 to 512
- target_ids: int32 [128, 512], P(('grp', 'row')), may hold values from 0 to 49999
- target_logq: bfloat16 [128, 512], P(('grp', 'row')), may hold values from -4 to 0
- negative_ids: int32 [2048], P(('grp', 'row')), may hold values from 0 to 49999
- negative_logq: bfloat16 [2048], P(('grp', 'row')), may hold values from -4 to 0
- table_weight: float32 [50000, 256], P('row'), may hold values from -0.6 to 0.6
- table_accum: float32 [50000], P('row'), may hold values from 1.1737531e-13 to 4.6950123e-13
- dense_weight: float32 [256, 4608], P(None, ('grp', 'row')), may hold values from -0.375 to 0.375
- dense_first: float32 [256, 4608], P(None, ('grp', 'row')), may hold values from -2.861023e-06 to 2.861023e-06
- dense_second: float32 [256, 4608], P(None, ('grp', 'row')), may hold values from 3.390842e-15 to 1.3563368e-14
- gain_weight: float32 [3, 256], replicated, may hold values from 0.5 to 1.5
- gain_first: float32 [3, 256], replicated, may hold values from -3.0517578e-05 to 3.0517578e-05
- gain_second: float32 [3, 256], replicated, may hold values from 3.390842e-13 to 1.3563368e-12
Outputs:
- mean_loss: float32 [], replicated
- grad_norm: float32 [], replicated
- new_table: float32 [50000, 256], P('row')
- table_grad: float32 [50000, 256], P('row')
- new_accum: float32 [50000], P('row')
- table_copy: bfloat16 [50000, 256], P('row')
- new_dense: float32 [256, 4608], P(None, ('grp', 'row'))
- new_first: float32 [256, 4608], P(None, ('grp', 'row'))
- new_second: float32 [256, 4608], P(None, ('grp', 'row'))
- dense_copy: bfloat16 [256, 4608], P(None, ('grp', 'row'))
- new_gains: float32 [3, 256], replicated
- new_gain_first: float32 [3, 256], replicated
- new_gain_second: float32 [3, 256], replicated
Inputs may be any that keep to these rules, and one draw needn't show every extreme that they name: `item_ids`: taking one device's item ids, target ids and negative ids together, at most 520 of them name rows with the same id // 3125; in each group some value of id // 3125 is named exactly 520 times by every device of the group.
All inputs are finite; a program needn't handle non-finite values.
Results may differ from a plain program's by a relative error of at most 0.0093.
The roundings to bfloat16 on the way count: a program that leaves them out, or rounds other values in their place, can miss the bound.
Values may be sent and summed in bfloat16 or wider, within the bound.
A program may use at most 256 MiB of HBM per device.

v0:
```python
import jax
import jax.numpy as jnp
from jax import lax
from jax.sharding import PartitionSpec as P

HEADS = 8
HDIM = 64
FF = 1024
STEP = 10
clip_level = 0.002
adam_rate = 0.05
gains_rate = 0.6
rows_rate = 0.05
beta_one = 0.9
beta_two = 0.999
adam_eps = 1e-08
decay_rate = 0.01


def in_blocks(array, dim, devices):
    shape = array.shape
    pieces = array.reshape(*shape[:dim], devices, shape[dim] // devices, *shape[dim + 1 :])
    return jnp.moveaxis(pieces, dim, 0)


def sum_at_owner(array, axis, dim):
    devices = lax.axis_size(axis)
    pieces = lax.all_to_all(in_blocks(array, dim, devices), axis, 0, 0, tiled=True)
    return jnp.sum(pieces.astype(jnp.float32), axis=0)


def norm_apply(values, gain):
    return values * lax.rsqrt(jnp.mean(values * values, -1, keepdims=True) + 1e-06) * gain


def gelu_apply(values):
    return jax.nn.gelu(values, approximate=True)


def adam_update(weight, first, second, grad, decay, rate):
    first_new = beta_one * first + (1.0 - beta_one) * grad
    second_new = beta_two * second + (1.0 - beta_two) * grad * grad
    fix_one = 1.0 - beta_one**STEP
    fix_two = 1.0 - beta_two**STEP
    weight_new = weight - rate * (
        first_new / fix_one / (jnp.sqrt(second_new / fix_two) + adam_eps) + decay * weight
    )
    return (weight_new, first_new, second_new)


def attention_probs(queries, keys_all):
    scores = (
        jnp.einsum("sqhd,skhd->shqk", queries, keys_all, preferred_element_type=jnp.float32) * 0.125
    )
    length = queries.shape[1]
    causal = lax.broadcasted_iota(jnp.int32, (length, length), 0) >= lax.broadcasted_iota(
        jnp.int32, (length, length), 1
    )
    scores = jnp.where(causal[None, None], scores, -1e30)
    exponent = jnp.exp(scores - jnp.max(scores, -1, keepdims=True))
    return exponent / jnp.sum(exponent, -1, keepdims=True)


def shards(
    item_ids,
    lengths,
    target_ids,
    target_logq,
    negative_ids,
    negative_logq,
    table_weight,
    table_accum,
    dense_weight,
    dense_first,
    dense_second,
    gain_weight,
    gain_first,
    gain_second,
):
    seq_dev, length = item_ids.shape
    rows_dev, model_width = table_weight.shape
    peer_count = lax.axis_size("row")
    inner = HEADS * HDIM
    tokens = seq_dev * length
    single_float = jnp.float32
    brain_float_half = jnp.bfloat16
    local_dense = dense_weight.astype(brain_float_half)
    full_dense = lax.all_gather(local_dense, ("grp", "row"), axis=1, tiled=True)
    query_key_value_weight = full_dense[:, : 3 * inner]
    output_weight = full_dense[:, 3 * inner : 4 * inner]
    up_weight = full_dense[:, 4 * inner : 4 * inner + FF]
    down_weight = full_dense[:, 4 * inner + FF : 4 * inner + 2 * FF]
    pos_rows = full_dense[:, 4 * inner + 2 * FF :].T.astype(single_float)
    requests = jnp.concatenate([item_ids.reshape(-1), target_ids.reshape(-1), negative_ids])
    capacity = 2 * requests.shape[0] // peer_count
    owners = requests // rows_dev
    one_hot = (owners[:, None] == jnp.arange(peer_count, dtype=jnp.int32)[None, :]).astype(
        jnp.int32
    )
    rank_in = jnp.sum((jnp.cumsum(one_hot, 0) - one_hot) * one_hot, 1)
    slot_at = owners * capacity + rank_in
    send_ids = jnp.full((peer_count * capacity,), -1, jnp.int32).at[slot_at].set(requests)
    send_ids = send_ids.reshape(peer_count, capacity)
    table_low = table_weight.astype(brain_float_half)
    row_base = lax.axis_index("row") * rows_dev
    asked_ids = lax.all_to_all(send_ids, "row", split_axis=0, concat_axis=0, tiled=True)
    present = asked_ids >= 0
    found_rows = table_low[jnp.where(present, asked_ids - row_base, 0)]
    found_rows = jnp.where(present[..., None], found_rows, jnp.zeros_like(found_rows))
    returned = lax.all_to_all(found_rows, "row", split_axis=0, concat_axis=0, tiled=True)
    fetched, asked_ids = (returned, asked_ids)
    picked = fetched.reshape(peer_count * capacity, model_width)[slot_at]
    hist_rows = picked[:tokens].reshape(seq_dev, length, model_width)
    target_rows = picked[tokens : 2 * tokens]
    own_negatives = picked[2 * tokens :]
    neg_rows, neg_bias = (
        lax.all_gather(own_negatives, "row", axis=0, tiled=True),
        lax.all_gather(negative_logq, "row", axis=0, tiled=True),
    )
    embedded_tokens = hist_rows.astype(single_float) + pos_rows[None]
    normed, norm_back_one = jax.vjp(norm_apply, embedded_tokens, gain_weight[0])
    normalized_narrow = normed.astype(brain_float_half)
    mixed_state = jnp.einsum(
        "rnq,qm->rnm",
        normalized_narrow,
        query_key_value_weight,
        preferred_element_type=single_float,
    ).astype(brain_float_half)
    queries = mixed_state[..., :inner].reshape(seq_dev, length, HEADS, HDIM)
    keys_all = mixed_state[..., inner : 2 * inner].reshape(seq_dev, length, HEADS, HDIM)
    values_all = mixed_state[..., 2 * inner :].reshape(seq_dev, length, HEADS, HDIM)
    attn_probs = attention_probs(queries, keys_all)
    probs_low = attn_probs.astype(brain_float_half)
    attention_context = jnp.einsum(
        "shqk,skhd->sqhd", probs_low, values_all, preferred_element_type=single_float
    )
    attention_context = attention_context.reshape(seq_dev, length, inner).astype(brain_float_half)
    after_attention_state = embedded_tokens + jnp.einsum(
        "xaj,oj->xao", attention_context, output_weight, preferred_element_type=single_float
    )
    normed_two, norm_back_two = jax.vjp(norm_apply, after_attention_state, gain_weight[1])
    second_normalized_narrow = normed_two.astype(brain_float_half)
    hidden_preactivation = jnp.einsum(
        "bvi,iq->bvq", second_normalized_narrow, up_weight, preferred_element_type=single_float
    )
    hidden, gaussian_unit_backward = jax.vjp(gelu_apply, hidden_preactivation)
    hidden_narrow = hidden.astype(brain_float_half)
    after_ffn = after_attention_state + jnp.einsum(
        "ixn,on->ixo", hidden_narrow, down_weight, preferred_element_type=single_float
    )
    states, norm_back_three = jax.vjp(norm_apply, after_ffn, gain_weight[2])
    states_low = states.astype(brain_float_half).reshape(tokens, model_width)
    states_full = states_low.astype(single_float)
    target_full = target_rows.astype(single_float)
    pos_logit = jnp.sum(states_full * target_full, -1) - target_logq.reshape(tokens).astype(
        single_float
    )
    neg_logit = (
        jnp.einsum("td,nd->tn", states_low, neg_rows, preferred_element_type=single_float)
        - neg_bias.astype(single_float)[None, :]
    )
    highest_logit = jnp.maximum(jnp.max(neg_logit, 1), pos_logit)
    log_total = highest_logit + jnp.log(
        jnp.exp(pos_logit - highest_logit) + jnp.sum(jnp.exp(neg_logit - highest_logit[:, None]), 1)
    )
    is_valid = lax.broadcasted_iota(jnp.int32, (seq_dev, length), 1) < lengths[:, None]
    valid_full = is_valid.reshape(tokens).astype(single_float)
    loss_local = jnp.sum(valid_full * (log_total - pos_logit))
    event_local = jnp.sum(valid_full)
    loss_total, event_total = lax.psum((loss_local, event_local), ("grp", "row"))
    inverse = 1.0 / event_total
    d_pos = valid_full * inverse * (jnp.exp(pos_logit - log_total) - 1.0)
    d_neg = (valid_full[:, None] * inverse * jnp.exp(neg_logit - log_total[:, None])).astype(
        brain_float_half
    )
    d_states = d_pos[:, None] * target_full + jnp.einsum(
        "tn,nd->td", d_neg, neg_rows, preferred_element_type=single_float
    )
    d_target = d_pos[:, None] * states_full
    neg_grad = sum_at_owner(
        jnp.einsum("tn,td->nd", d_neg, states_low, preferred_element_type=single_float).astype(
            jnp.bfloat16
        ),
        "row",
        0,
    )
    d_ffn, d_gain_three = norm_back_three(d_states.reshape(seq_dev, length, model_width))
    branch_gradient = d_ffn.astype(brain_float_half)
    down_weight_gradient = jnp.einsum(
        "qgp,qgv->pv", branch_gradient, hidden_narrow, preferred_element_type=single_float
    )
    (hidden_gradient,) = gaussian_unit_backward(
        jnp.einsum("bvi,iq->bvq", branch_gradient, down_weight, preferred_element_type=single_float)
    )
    hidden_gradient_narrow = hidden_gradient.astype(brain_float_half)
    up_weight_gradient = jnp.einsum(
        "qgp,qgv->pv",
        second_normalized_narrow,
        hidden_gradient_narrow,
        preferred_element_type=single_float,
    )
    d_attn_part, d_gain_two = norm_back_two(
        jnp.einsum(
            "ixn,on->ixo", hidden_gradient_narrow, up_weight, preferred_element_type=single_float
        )
    )
    d_attn = d_ffn + d_attn_part
    output_gradient_narrow = d_attn.astype(brain_float_half)
    output_weight_gradient = jnp.einsum(
        "nkg,nka->ga",
        output_gradient_narrow,
        attention_context,
        preferred_element_type=single_float,
    )
    context_gradient = jnp.einsum(
        "mbg,gr->mbr", output_gradient_narrow, output_weight, preferred_element_type=single_float
    ).astype(brain_float_half)
    context_gradient = context_gradient.reshape(seq_dev, length, HEADS, HDIM)
    d_values = jnp.einsum(
        "shqk,sqhd->skhd", probs_low, context_gradient, preferred_element_type=single_float
    )
    d_probs = jnp.einsum(
        "sqhd,skhd->shqk", context_gradient, values_all, preferred_element_type=single_float
    )
    d_scores = (attn_probs * (d_probs - jnp.sum(attn_probs * d_probs, -1, keepdims=True))).astype(
        brain_float_half
    )
    d_queries = (
        jnp.einsum("shqk,skhd->sqhd", d_scores, keys_all, preferred_element_type=single_float)
        * 0.125
    )
    d_keys = (
        jnp.einsum("shqk,sqhd->skhd", d_scores, queries, preferred_element_type=single_float)
        * 0.125
    )
    mixed_gradient = jnp.concatenate(
        [
            d_queries.reshape(seq_dev, length, inner),
            d_keys.reshape(seq_dev, length, inner),
            d_values.reshape(seq_dev, length, inner),
        ],
        -1,
    ).astype(brain_float_half)
    query_key_value_gradient = jnp.einsum(
        "rbp,rbg->pg", normalized_narrow, mixed_gradient, preferred_element_type=single_float
    )
    d_embed_part, d_gain_one = norm_back_one(
        jnp.einsum(
            "igp,zp->igz",
            mixed_gradient,
            query_key_value_weight,
            preferred_element_type=single_float,
        )
    )
    d_embedded = d_attn + d_embed_part
    grad_pos = jnp.sum(d_embedded, 0).T
    grad_local = jnp.concatenate(
        [
            query_key_value_gradient,
            output_weight_gradient,
            up_weight_gradient,
            down_weight_gradient,
            grad_pos,
        ],
        1,
    )
    gain_local = jnp.stack([d_gain_one, d_gain_two, d_gain_three])
    dense_grad = lax.psum_scatter(grad_local, ("grp", "row"), scatter_dimension=1, tiled=True)
    row_grads = jnp.concatenate([d_embedded.reshape(tokens, model_width), d_target, neg_grad], 0)
    sent_grads = (
        jnp.zeros((peer_count * capacity, model_width), single_float).at[slot_at].set(row_grads)
    )
    arrived = lax.all_to_all(
        sent_grads.reshape(peer_count, capacity, model_width).astype(jnp.bfloat16),
        "row",
        split_axis=0,
        concat_axis=0,
        tiled=True,
    ).astype(jnp.float32)
    present = asked_ids >= 0
    local_rows = jnp.where(present, asked_ids - row_base, 0).reshape(-1)
    arrived = jnp.where(present[..., None], arrived, 0.0).reshape(-1, model_width)
    owner_grad = jax.ops.segment_sum(arrived, local_rows, num_segments=rows_dev)
    table_full = lax.psum(owner_grad.astype(jnp.bfloat16), "grp").astype(jnp.float32)
    dense_sq = jnp.sum(dense_grad * dense_grad)
    table_sq = jnp.sum(table_full * table_full) / lax.axis_size("grp")
    gain_grad, dense_total, table_total = lax.psum((gain_local, dense_sq, table_sq), ("grp", "row"))
    raw_norm = jnp.sqrt(dense_total + table_total + jnp.sum(gain_grad * gain_grad))
    factor = jnp.minimum(1.0, clip_level / raw_norm)
    table_grad = table_full * factor
    new_accum = table_accum + jnp.mean(table_grad * table_grad, -1)
    new_table = table_weight - rows_rate * table_grad / (jnp.sqrt(new_accum)[:, None] + adam_eps)
    new_dense, new_first, new_second = adam_update(
        dense_weight, dense_first, dense_second, dense_grad * factor, decay_rate, adam_rate
    )
    new_gains, new_gain_first, new_gain_second = adam_update(
        gain_weight, gain_first, gain_second, gain_grad * factor, 0.0, gains_rate
    )
    mean_loss = loss_total / event_total
    return (
        mean_loss,
        raw_norm,
        new_table,
        table_grad,
        new_accum,
        new_table.astype(brain_float_half),
        new_dense,
        new_first,
        new_second,
        new_dense.astype(brain_float_half),
        new_gains,
        new_gain_first,
        new_gain_second,
    )


def solution(mesh):
    return jax.shard_map(
        shards,
        mesh=mesh,
        in_specs=(
            P(("grp", "row"), None),
            P(("grp", "row")),
            P(("grp", "row"), None),
            P(("grp", "row"), None),
            P(("grp", "row")),
            P(("grp", "row")),
            P("row", None),
            P("row"),
            P(None, ("grp", "row")),
            P(None, ("grp", "row")),
            P(None, ("grp", "row")),
            P(),
            P(),
            P(),
        ),
        out_specs=(
            P(),
            P(),
            P("row", None),
            P("row", None),
            P("row"),
            P("row", None),
            P(None, ("grp", "row")),
            P(None, ("grp", "row")),
            P(None, ("grp", "row")),
            P(None, ("grp", "row")),
            P(),
            P(),
            P(),
        ),
        check_vma=False,
    )
```

profile of v0, /device:TPU:0, one launch (start us, length us, event | category | flops | bytes accessed | tf_op | source)
XLA Modules:
  0.0 841.4 jit_solution(8096171434932233010)
XLA Ops:
  10.8 4.7 reduce-window.6
  16.7 20.6 %scatter_custom_fusion = s32[8320]{0:T(1024)S(1)} fusion(s32[4160]{0:T(1024)S(1)} %fusion.57, s32[4160]{0:T(1024)S(1)} %constant_dynamic-update-slice_fusion.1, s32[]{:T(128)} %constant.34.clone.1), kind=kCustom, calls=%fused_computation.133 | custom fusion | bytes 33284 | tf_op jit(solution)/shard_map/scatter | solution.py:102
  38.0 7.4 all-to-all-start
  47.5 4.6 all-to-all-done
  52.8 24.2 %gather_fusion = bf16[8320,256]{1,0:T(8,128)(2,1)} fusion(bf16[3125,256]{1,0:T(8,128)(2,1)S(1)} %convert_element_type.132, s32[9216]{0:T(1024)S(1)} %pad_clamp_fusion), kind=kCustom, calls=%fused_computation | custom fusion | bytes 8552960 | tf_op jit(solution)/shard_map/gather | solution.py:108
  77.7 5.3 broadcast_select_fusion
  83.0 4.7 all-to-all-start.1
  89.9 99.9 %all-reduce.1 = bf16[1024]{0:T(1024)(128)(2,1)S(1)} all-reduce(bf16[1024]{0:T(1024)(128)(2,1)S(1)} %dynamic-update-slice), channel_id=1, replica_groups=mesh['grp'=2,'row'=16] {'row'}, use_global_device_ids=true, to_apply=%add.1 | all-reduce | flops 1024 | bytes 4096
  191.0 12.5 %gather_fusion.1 = bf16[4160,256]{1,0:T(8,128)(2,1)S(1)} fusion(bf16[8320,256]{1,0:T(8,128)(2,1)} %bitcast.5, s32[5120]{0:T(1024)S(1)} %pad_clamp_fusion.1), kind=kCustom, calls=%fused_computation.1 | custom fusion | bytes 4276480 | tf_op jit(solution)/shard_map/gather | solution.py:112
  205.6 40.4 %all_gather.10 = bf16[1024,256]{1,0:T(8,128)(2,1)} all-gather(bf16[64,256]{1,0:T(8,128)(2,1)S(1)} %slice.84), channel_id=1, replica_groups=mesh['grp'=2,'row'=16] {'row'}, dimensions={0}, use_global_device_ids=true | all-gather | bytes 557056 | tf_op jit(solution)/shard_map/all_gather | solution.py:117
  246.1 3.2 convolution_convert_fusion
  249.3 2.9 fusion.70
  255.0 4.6 copy.150
  259.6 4.1 copy.149
  263.7 19.1 %fusion.72 = (f32[4,8,512]{2,1,0:T(8,128)S(1)}, f32[4,8,512,512]{2,3,1,0:T(8,128)}) fusion(pred[512,512]{0,1:T(8,128)(4,1)S(1)} %iota_compare_fusion, bf16[4,512,8,64]{1,3,2,0:T(8,128)(2,1)} %bitcast.183, bf16[4,512,8,64]{1,3,2,0:T(8,128)(2,1)S(1)} %bitcast.181), kind=kOutput, calls=%fused_computation.173 | convolution fusion | flops 1107296768 | bytes 38076416 | tf_op jit(solution)/shard_map/sub | solution.py:60
  282.8 14.4 %fusion.33 = bf16[4,8,64,512]{3,2,1,0:T(8,128)(2,1)} fusion(bf16[4,512,8,64]{1,3,2,0:T(8,128)(2,1)} %bitcast.193, f32[4,8,512,512]{2,3,1,0:T(8,128)} %get-tuple-element.102, f32[4,8,512]{2,1,0:T(8,128)S(1)} %get-tuple-element.101), kind=kOutput, calls=%fused_computation.78 | convolution fusion | flops 1091567616 | bytes 37814272 | tf_op jit(solution)/shard_map/shqk,skhd->sqhd/dot_general | solution.py:134
  297.2 3.3 multiply_reduce_fusion.9
  302.9 4.5 multiply_reduce_fusion.8
  310.7 5.5 subtract_reduce_fusion
  316.2 4.3 exponential_reduce_fusion
  321.2 38.9 %psum.43 = f32[]{:T(128)} all-reduce(f32[]{:T(128)} %get-tuple-element.71), channel_id=1, replica_groups=mesh['grp'=2,'row'=16] {'grp','row'}, use_global_device_ids=true, to_apply=%region_15.16 | all-reduce | flops 1 | bytes 8 | tf_op jit(solution)/shard_map/psum | solution.py:170
  360.9 4.4 multiply_convert_fusion.1
  373.8 6.7 fusion.11
  387.8 15.3 %fusion.36 = bf16[4,8,64,512]{3,2,1,0:T(8,128)(2,1)} fusion(bf16[4,512,8,64]{1,3,2,0:T(8,128)(2,1)} %bitcast.196, f32[4,8,512,512]{2,3,1,0:T(8,128)} %get-tuple-element.102, f32[4,8,512]{2,1,0:T(8,128)S(1)} %get-tuple-element.101), kind=kOutput, calls=%fused_computation.79 | convolution fusion | flops 1091567616 | bytes 37814272 | tf_op jit(solution)/shard_map/shqk,sqhd->skhd/dot_general | solution.py:219
  403.1 22.9 %multiply_reduce_fusion = (f32[4,8,512]{2,1,0:T(8,128)S(1)}, f32[4,8,512,512]{2,3,1,0:T(8,128)}) fusion(f32[4,8,512,512]{2,3,1,0:T(8,128)} %get-tuple-element.102, f32[4,8,512]{2,1,0:T(8,128)S(1)} %get-tuple-element.101, bf16[4,512,8,64]{1,3,2,0:T(8,128)(2,1)} %bitcast.197, bf16[4,512,8,64]{1,3,2,0:T(8,128)(2,1)} %bitcast.194), kind=kOutput, calls=%fused_computation.7 | convolution fusion | flops 1098891264 | bytes 71434240 | tf_op jit(solution)/shard_map/sqhd,skhd->shqk/dot_general | solution.py:222
  426.0 27.6 %multiply_convert_fusion = bf16[4,8,512,512]{2,3,1,0:T(8,128)(2,1)} fusion(f32[4,8,512,512]{2,3,1,0:T(8,128)} %get-tuple-element.111, f32[4,8,512]{2,1,0:T(8,128)S(1)} %get-tuple-element.110, f32[4,8,512,512]{2,3,1,0:T(8,128)} %get-tuple-element.102, f32[4,8,512]{2,1,0:T(8,128)S(1)} %get-tuple-element.101), kind=kLoop, calls=%fused_computation.6 | loop fusion | flops 33554432 | bytes 84017152 | tf_op jit(solution)/shard_map/convert_element_type | solution.py:225
  453.6 12.9 %multiply_convert_fusion.3 = bf16[4,8,64,512]{3,2,1,0:T(8,128)(2,1)} fusion(bf16[4,512,8,64]{1,3,2,0:T(8,128)(2,1)} %bitcast.184, bf16[4,8,512,512]{2,3,1,0:T(8,128)(2,1)} %multiply_convert_fusion), kind=kOutput, calls=%fused_computation.43 | convolution fusion | flops 1075838976 | bytes 20971520 | tf_op jit(solution)/shard_map/shqk,sqhd->skhd/dot_general | solution.py:233
  466.5 10.6 %multiply_convert_fusion.4 = bf16[4,8,64,512]{3,2,1,0:T(8,128)(2,1)} fusion(bf16[4,512,8,64]{1,3,2,0:T(8,128)(2,1)} %bitcast.182, bf16[4,8,512,512]{2,3,1,0:T(8,128)(2,1)} %multiply_convert_fusion), kind=kOutput, calls=%fused_computation.44 | convolution fusion | flops 1075838976 | bytes 20971520 | tf_op jit(solution)/shard_map/shqk,skhd->sqhd/dot_general | solution.py:229
  477.1 5.4 all-to-all-start.2
  482.5 4.1 copy.163
  486.6 4.2 copy.161
  490.8 4.2 copy.162
  495.0 5.4 multiply_reduce_fusion.4
  500.5 2.8 fusion.30
  507.2 6.3 fusion.26
  514.6 27.3 %scatter_custom_fusion.1 = f32[8320,256]{1,0:T(8,128)} fusion(s32[4160]{0:T(1024)} %copy-done.28, f32[64,256]{1,0:T(8,128)S(1)} %convert_reduce_fusion, f32[]{:T(128)} %constant.48.clone.1, f32[2048,256]{1,0:T(8,128)} %convert_multiply_fusion.4, f32[2048,256]{1,0:T(8,128)} %bitcast.174, f32[]{:T(128)} %constant.43.clone.1), kind=kCustom, calls=%fused_computation.35 | custom fusion | flops 2129920 | bytes 12780544 | tf_op jit(solution)/shard_map/scatter | solution.py:271
  541.9 5.3 convert_element_type.163
  547.2 6.1 all-to-all-start.3
  553.4 4.0 fusion.43
  559.8 7.6 fusion.41
  568.3 6.0 copy.183
  575.2 63.3 %all-to-all-done.3 = bf16[16,520,256]{2,1,0:T(8,128)(2,1)} async-done(((bf16[16,520,256]{2,1,0:T(8,128)(2,1)}), bf16[16,520,256]{2,1,0:T(8,128)(2,1)}, u32[]{:S(2)}, u32[]{:S(2)}) %all-to-all-start.3) | async-done | bytes 4259872 | tf_op jit(solution)/shard_map/all_to_all | solution.py:273
  638.5 7.1 convert_select_fusion
  645.6 52.6 %scatter_custom_fusion.2 = f32[3125,256]{1,0:T(8,128)S(1)} fusion(s32[8320]{0:T(1024)S(1)} %reshape.563, f32[8320,256]{1,0:T(8,128)} %bitcast.180, f32[]{:T(128)} %constant.43.clone.1), kind=kCustom, calls=%fused_computation.82 | custom fusion | flops 2129920 | bytes 3200512 | tf_op jit(solution)/shard_map/scatter-add | solution.py:283
  701.4 76.3 %all-reduce.5.cloned.1.call-done = bf16[3125,256]{1,0:T(8,128)(2,1)} async-done(((bf16[3125,256]{1,0:T(8,128)(2,1)}), bf16[3125,256]{1,0:T(8,128)(2,1)}) %all-reduce.5.cloned.1.call-update) | async-done | bytes 1600016 | tf_op jit(solution)/shard_map/psum | solution.py:284
  777.7 3.0 fusion.25
  782.0 39.6 %all-reduce.2 = (f32[]{:T(128)}, f32[]{:T(128)}, f32[3,256]{1,0:T(4,128)S(1)}) all-reduce(f32[]{:T(128)} %get-tuple-element.72, f32[]{:T(128)S(6)} %add.230, f32[3,256]{1,0:T(4,128)S(1)} %pad_maximum_fusion.3), channel_id=1, replica_groups=mesh['grp'=2,'row'=16] {'grp','row'}, use_global_device_ids=true, to_apply=%region_13.14 | all-reduce | flops 770 | bytes 6160 | tf_op jit(solution)/shard_map/psum | solution.py:170
  828.6 3.0 fusion.68
  (188 shorter events, 55.8 us)
Async XLA Ops:
  7.2 9.3 %copy-start.44 = (s32[64]{0:T(128)S(1)}, s32[64]{0:T(128)}, u32[]{:S(2)}) copy-start(s32[64]{0:T(128)} %param.18) | copy-start | bytes 772
  16.7 173.2 %copy-start.28 = (s32[4160]{0:T(1024)}, s32[4160]{0:T(1024)S(1)}, u32[]{:S(2)}) copy-start(s32[4160]{0:T(1024)S(1)} %fusion.57) | copy-start | bytes 49924
  38.0 14.1 %all-to-all-start = ((s32[16,1,520]{2,1,0:T(1,128)}), s32[16,1,520]{2,1,0:T(1,128)S(1)}, u32[]{:S(2)}, u32[]{:S(2)}) async-start(s32[16,1,520]{2,1,0:T(1,128)} %all_to_all.15), calls=%async_computation | async-start | bytes 81920 | tf_op jit(solution)/shard_map/all_to_all | solution.py:106
  83.0 4.8 copy-start.21
  83.0 5.5 copy-start.46
  83.0 6.7 copy-start.45
  83.0 106.9 %copy-start.34 = (bf16[4,512]{1,0:T(4,128)(2,1)S(1)}, bf16[4,512]{1,0:T(4,128)(2,1)}, u32[]{:S(2)}) copy-start(bf16[4,512]{1,0:T(4,128)(2,1)} %param.17) | copy-start | bytes 12292
  83.0 107.0 %copy-start.35 = (f32[3,256]{1,0:T(4,128)S(1)}, f32[3,256]{1,0:T(4,128)}, u32[]{:S(2)}) copy-start(f32[3,256]{1,0:T(4,128)} %param.25) | copy-start | bytes 9220
  83.0 108.0 %all-to-all-start.1 = ((bf16[16,520,256]{2,1,0:T(8,128)(2,1)}), bf16[16,520,256]{2,1,0:T(8,128)(2,1)}, u32[]{:S(2)}, u32[]{:S(2)}) async-start(bf16[16,520,256]{2,1,0:T(8,128)(2,1)} %broadcast_select_fusion), calls=%async_computation.1 | async-start | bytes 8519680 | tf_op jit(solution)/shard_map/all_to_all | solution.py:110
  87.7 102.3 %all-gather.2.cloned.1.call-start = ((), (), s32[]{:S(2)}) async-start(), calls=%async_computation.5 | async-start | bytes 2433024 | tf_op jit(solution)/shard_map/all_gather | solution.py:88
  190.0 56.1 %copy-start.37 = (f32[1,256]{1,0:T(1,128)}, f32[1,256]{1,0:T(1,128)S(1)}, u32[]{:S(2)}) copy-start(f32[1,256]{1,0:T(1,128)S(1)} %get-tuple-element.100) | copy-start | bytes 3076
  191.0 106.2 %copy-start.9 = (f32[512,256]{1,0:T(8,128)}, f32[512,256]{1,0:T(8,128)S(1)}, u32[]{:S(2)}) copy-start(f32[512,256]{1,0:T(8,128)S(1)} %convert_bitcast_fusion) | copy-start | bytes 1572868
  203.6 42.5 %copy-start.2 = (bf16[4160,256]{1,0:T(8,128)(2,1)}, bf16[4160,256]{1,0:T(8,128)(2,1)S(1)}, u32[]{:S(2)}) copy-start(bf16[4160,256]{1,0:T(8,128)(2,1)S(1)} %gather_fusion.1) | copy-start | bytes 6389764
  205.6 43.7 %copy-start.29 = (f32[4,512]{1,0:T(4,128)}, f32[4,512]{1,0:T(4,128)S(1)}, u32[]{:S(2)}) copy-start(f32[4,512]{1,0:T(4,128)S(1)} %add.216) | copy-start | bytes 24580
  205.6 43.7 %copy-start.31 = (f32[4,512]{1,0:T(4,128)}, f32[4,512]{1,0:T(4,128)S(1)}, u32[]{:S(2)}) copy-start(f32[4,512]{1,0:T(4,128)S(1)} %rsqrt.30) | copy-start | bytes 24580
  255.0 8.7 %copy-start.15 = (bf16[4,512,512]{1,2,0:T(8,128)(2,1)}, bf16[4,512,512]{1,2,0:T(8,128)(2,1)S(1)}, u32[]{:S(2)}) copy-start(bf16[4,512,512]{1,2,0:T(8,128)(2,1)S(1)} %copy.151) | copy-start | bytes 6291460
  302.9 4.5 copy-start.16
  316.2 4.3 copy-start.42
  365.4 2.1 copy-start.3
  365.4 2.1 copy-start.18
  365.4 8.0 slice-start
  367.5 5.9 slice-start.1
  369.0 13.8 %copy-start.7 = (f32[2048,256]{1,0:T(8,128)}, f32[2048,256]{1,0:T(8,128)S(1)}, u32[]{:S(2)}) copy-start(f32[2048,256]{1,0:T(8,128)S(1)} %convolution_add_fusion) | copy-start | bytes 6291460
  369.1 3.1 copy-start.5
  380.5 2.3 copy-start.13
  477.1 36.4 %all-to-all-start.2 = ((bf16[16,64,256]{2,1,0:T(8,128)(2,1)}), bf16[16,64,256]{2,1,0:T(8,128)(2,1)}, u32[]{:S(2)}, u32[]{:S(2)}) async-start(bf16[16,64,256]{2,1,0:T(8,128)(2,1)} %bitcast.39), calls=%async_computation.2 | async-start | bytes 1048576 | tf_op jit(solution)/shard_map/all_to_all | solution.py:28
  490.8 4.2 copy-start.10
  490.8 4.2 copy-start.32
  490.8 4.2 copy-start.38
  495.0 5.5 copy-start.30
  495.0 5.5 copy-start.1
  547.2 91.3 %all-to-all-start.3 = ((bf16[16,520,256]{2,1,0:T(8,128)(2,1)}), bf16[16,520,256]{2,1,0:T(8,128)(2,1)}, u32[]{:S(2)}, u32[]{:S(2)}) async-start(bf16[16,520,256]{2,1,0:T(8,128)(2,1)} %bitcast.179), calls=%async_computation.3 | async-start | bytes 8519680 | tf_op jit(solution)/shard_map/all_to_all | solution.py:273
  553.3 146.3 %reduce-scatter.4.cloned.1.call-start = ((), (), s32[]{:S(2)}) async-start(), calls=%async_computation.7 | async-start | bytes 4866048
  553.4 4.0 copy-start.14
  557.4 2.4 copy-start.6
  557.4 2.4 copy-start.8
  574.3 64.2 %copy-start.27 = (pred[16,520]{1,0:T(8,128)(4,1)S(1)}, pred[16,520]{1,0:T(8,128)(4,1)}, u32[]{:S(2)}) copy-start(pred[16,520]{1,0:T(8,128)(4,1)} %copy-done.26) | copy-start | bytes 24964
  574.3 203.4 %all-reduce.5.cloned.1.call-start = ((), (), s32[]{:S(2)}) async-start(), calls=%async_computation.6 | async-start | bytes 3203072 | tf_op jit(solution)/shard_map/psum | solution.py:284
  699.6 125.3 %copy-start.36 = (f32[3,256]{1,0:T(4,128)S(1)}, f32[3,256]{1,0:T(4,128)}, u32[]{:S(2)}) copy-start(f32[3,256]{1,0:T(4,128)} %param.25) | copy-start | bytes 9220
  699.6 125.3 %copy-start.40 = (f32[3,256]{1,0:T(4,128)S(1)}, f32[3,256]{1,0:T(4,128)}, u32[]{:S(2)}) copy-start(f32[3,256]{1,0:T(4,128)} %param.26) | copy-start | bytes 9220
  699.6 125.3 %copy-start.41 = (f32[3,256]{1,0:T(4,128)S(1)}, f32[3,256]{1,0:T(4,128)}, u32[]{:S(2)}) copy-start(f32[3,256]{1,0:T(4,128)} %param.27) | copy-start | bytes 9220
  777.7 47.8 %copy-start.17 = (bf16[3125,256]{1,0:T(8,128)(2,1)S(1)}, bf16[3125,256]{1,0:T(8,128)(2,1)}, u32[]{:S(2)}) copy-start(bf16[3125,256]{1,0:T(8,128)(2,1)} %all-reduce.5.cloned.1.call-done) | copy-start | bytes 4800004
  825.5 3.0 copy-start.11
  826.1 5.5 copy-start.12
  828.5 3.0 copy-start.20
  828.5 3.0 copy-start.22
  828.5 3.0 copy-start.24
  828.6 3.0 copy-start.25
  (8 other events, 9.2 us)
Sparse Core Ops, SparseCore 0:
  92.0 97.0 all-gather.1
  574.4 113.9 reduce-scatter.3
  699.7 77.9 all-reduce.4
where the time goes:
time: 849 us; the launch traced here: 841 us
  blocking collectives  219 us (26%)
  other arithmetic  171 us (20%)
  matrix products  154 us (18%)
  waiting for transfers between devices  144 us (17%)
  local copies, waits for them, and re-layouts  107 us (13%)
  starting transfers between devices  23.7 us (3%)
  between operations  22.5 us (3%)
    unnamed x1, blocking collectives  99.9 us
    psum x2, blocking collectives, shards(): lax.psum((loss_local, event_local), ('grp', 'row'))  78.5 us
    psum x1, waiting for transfers between devices, shards(): lax.psum(owner_grad.astype(jnp.bfloat16), 'grp').astype(jnp.float32)  76.3 us
    all_to_all x1, waiting for transfers between devices, shards(): lax.all_to_all(sent_grads.reshape(peer_count, capacity, model_width).asty...  63.3 us
    scatter-add x1, other arithmetic, shards(): owner_grad = jax.ops.segment_sum(arrived, local_rows, num_segments=rows_dev)  52.6 us
    all_gather x1, blocking collectives, shards(): lax.all_gather(own_negatives, 'row', axis=0, tiled=True)  40.4 us
    convert_element_type x1, other arithmetic, shards(): (attn_probs * (d_probs - jnp.sum(attn_probs * d_probs, -1, keepdims=True)...  27.6 us
    scatter x1, other arithmetic, shards(): jnp.zeros((peer_count * capacity, model_width), single_float).at[slot_at]  27.3 us
  transfers between devices with their start and end apart: 7, of which 3 were waited for; matrix products, arithmetic and copies ran while one was open for 14% of the time, Pallas kernels for 0%

commit v1 on v0

--- a/solution.py
+++ b/solution.py
@@ -1,3 +1,4 @@
+import functools
 import jax
 import jax.numpy as jnp
 from jax import lax
@@ -15,6 +16,28 @@
 beta_two = 0.999
 adam_eps = 1e-08
 decay_rate = 0.01
+
+
+def reach_the_loads(piece_in, at_axis):
+    piece_in = jnp.moveaxis(piece_in, 0, at_axis)
+    seen_now = piece_in.shape
+    return piece_in.reshape(
+        *seen_now[:at_axis], seen_now[at_axis] * seen_now[at_axis + 1], *seen_now[at_axis + 2 :]
+    )
+
+
+def name_sheets_by_axis(local_values, device_axis, dim_no):
+    workers = lax.psum(1, device_axis)
+    blocks_here = [local_values]
+    pool = [(it, (it + 1) % workers) for it in range(workers)]
+    while len(blocks_here) < workers:
+        blocks_here.append(lax.ppermute(blocks_here[-1], device_axis, pool))
+    known = lax.axis_index(device_axis)
+    blocks_here = jnp.stack(blocks_here, 0)[(known - jnp.arange(workers)) % workers]
+    return reach_the_loads(blocks_here, dim_no)
+
+
+proceed_table = functools.partial(name_sheets_by_axis, device_axis="row", dim_no=0)
 
 
 def in_blocks(array, dim, devices):
@@ -114,7 +137,7 @@
     target_rows = picked[tokens : 2 * tokens]
     own_negatives = picked[2 * tokens :]
     neg_rows, neg_bias = (
-        lax.all_gather(own_negatives, "row", axis=0, tiled=True),
+        proceed_table(own_negatives),
         lax.all_gather(negative_logq, "row", axis=0, tiled=True),
     )
     embedded_tokens = hist_rows.astype(single_float) + pos_rows[None]

time: 849 us -> 911 us (1.073)
  waiting for transfers between devices: 144 us -> 218 us
  blocking collectives: 219 us -> 177 us
  starting transfers between devices: 23.7 us -> 42.2 us
  local copies, waits for them, and re-layouts: 107 us -> 120 us
    ppermute x0 -> x15, waiting for transfers between devices: none -> 73.5 us  [name_sheets_by_axis(): blocks_here.append(lax.ppermute(blocks_here[-1], device_axis, pool))]
    all_gather x1 -> x0, blocking collectives: 40.4 us -> none  [shards(): lax.all_gather(own_negatives, 'row', axis=0, tiled=True)]
    ppermute x0 -> x15, starting transfers between devices: none -> 17.3 us  [name_sheets_by_axis(): blocks_here.append(lax.ppermute(blocks_here[-1], device_axis, pool))]
    unnamed x112 -> x129, local copies, waits for them, and re-layouts: 18.7 us -> 28.6 us
  transfers between devices with their start and end apart: 7 -> 22, of which waited for: 3 -> 17; matrix products, arithmetic and copies ran while one was open for 14% -> 21% of each run, Pallas kernels for 0% -> 0%
where the time goes in v1:
time: 911 us; the launch traced here: 904 us
  waiting for transfers between devices  218 us (24%)
  blocking collectives  177 us (19%)
  other arithmetic  169 us (19%)
  matrix products  155 us (17%)
  local copies, waits for them, and re-layouts  120 us (13%)
  starting transfers between devices  42.2 us (5%)
  between operations  22.5 us (2%)
    unnamed x1, blocking collectives  99.9 us
    psum x1, waiting for transfers between devices, shards(): lax.psum(owner_grad.astype(jnp.bfloat16), 'grp').astype(jnp.float32)  77.2 us
    psum x2, blocking collectives, shards(): lax.psum((loss_local, event_local), ('grp', 'row'))  76.8 us
    ppermute x15, waiting for transfers between devices, name_sheets_by_axis(): blocks_here.append(lax.ppermute(blocks_here[-1], device_axis, pool))  73.5 us
    all_to_all x1, waiting for transfers between devices, shards(): lax.all_to_all(sent_grads.reshape(peer_count, capacity, model_width).asty...  62.8 us
    scatter-add x1, other arithmetic, shards(): owner_grad = jax.ops.segment_sum(arrived, local_rows, num_segments=rows_dev)  52.6 us
    unnamed x129, local copies, waits for them, and re-layouts  28.6 us
    convert_element_type x1, other arithmetic, shards(): (attn_probs * (d_probs - jnp.sum(attn_probs * d_probs, -1, keepdims=True)...  27.6 us
  transfers between devices with their start and end apart: 22, of which 17 were waited for; matrix products, arithmetic and copies ran while one was open for 21% of the time, Pallas kernels for 0%

profile of v1, /device:TPU:0, one launch (start us, length us, event | category | flops | bytes accessed | tf_op | source)
XLA Modules:
  0.0 903.5 jit_solution(14629749971432632154)
XLA Ops:
  10.8 4.7 reduce-window.6
  16.7 20.6 %scatter_custom_fusion = s32[8320]{0:T(1024)S(1)} fusion(s32[4160]{0:T(1024)S(1)} %fusion.57, s32[4160]{0:T(1024)S(1)} %constant_dynamic-update-slice_fusion.17, s32[]{:T(128)} %constant.36.clone.1), kind=kCustom, calls=%fused_computation.151 | custom fusion | bytes 33284 | tf_op jit(solution)/shard_map/scatter | solution.py:125
  38.0 7.4 all-to-all-start
  47.5 4.6 all-to-all-done
  52.8 24.2 %gather_fusion = bf16[8320,256]{1,0:T(8,128)(2,1)} fusion(bf16[3125,256]{1,0:T(8,128)(2,1)S(1)} %convert_element_type.132, s32[9216]{0:T(1024)S(1)} %pad_clamp_fusion), kind=kCustom, calls=%fused_computation | custom fusion | bytes 8552960 | tf_op jit(solution)/shard_map/gather | solution.py:131
  77.7 5.3 broadcast_select_fusion
  83.0 4.7 all-to-all-start.1
  89.9 99.9 %all-reduce.1 = bf16[1024]{0:T(1024)(128)(2,1)S(1)} all-reduce(bf16[1024]{0:T(1024)(128)(2,1)S(1)} %dynamic-update-slice), channel_id=1, replica_groups=mesh['grp'=2,'row'=16] {'row'}, use_global_device_ids=true, to_apply=%add.1 | all-reduce | flops 1024 | bytes 4096
  191.1 12.5 %gather_fusion.1 = bf16[4160,256]{1,0:T(8,128)(2,1)S(1)} fusion(bf16[8320,256]{1,0:T(8,128)(2,1)} %bitcast.5, s32[5120]{0:T(1024)S(1)} %pad_clamp_fusion.1), kind=kCustom, calls=%fused_computation.1 | custom fusion | bytes 4276480 | tf_op jit(solution)/shard_map/gather | solution.py:135
  205.6 15.0 %collective-permute-start = (bf16[64,256]{1,0:T(8,128)(2,1)S(1)}, bf16[64,256]{1,0:T(8,128)(2,1)S(1)}, u32[]{:S(2)}, u32[]{:S(2)}) collective-permute-start(bf16[64,256]{1,0:T(8,128)(2,1)S(1)} %slice.86), channel_id=1, source_target_pairs={{0,1},{1,2},{2,3},{3,4},{4,5},{5,6},{6,7},{7,8},{8,9},{9,10},{10,1... | collective-permute-start | bytes 98312 | tf_op jit(solution)/shard_map/ppermute | solution.py:34
  229.6 4.6 copy.150
  238.3 19.1 %fusion.74 = (f32[4,8,512]{2,1,0:T(8,128)S(1)}, f32[4,8,512,512]{2,3,1,0:T(8,128)}) fusion(pred[512,512]{0,1:T(8,128)(4,1)S(1)} %iota_compare_fusion, bf16[4,512,8,64]{1,3,2,0:T(8,128)(2,1)} %bitcast.218, bf16[4,512,8,64]{1,3,2,0:T(8,128)(2,1)S(1)} %bitcast.216), kind=kOutput, calls=%fused_computation.197 | convolution fusion | flops 1107296768 | bytes 38076416 | tf_op jit(solution)/shard_map/sub | solution.py:83
  257.4 14.7 %fusion.33 = bf16[4,8,64,512]{3,2,1,0:T(8,128)(2,1)} fusion(bf16[4,512,8,64]{1,3,2,0:T(8,128)(2,1)} %bitcast.230, f32[4,8,512,512]{2,3,1,0:T(8,128)} %get-tuple-element.102, f32[4,8,512]{2,1,0:T(8,128)S(1)} %get-tuple-element.101), kind=kOutput, calls=%fused_computation.79 | convolution fusion | flops 1091567616 | bytes 37814272 | tf_op jit(solution)/shard_map/shqk,skhd->sqhd/dot_general | solution.py:157
  277.8 4.5 multiply_reduce_fusion.8
  292.4 5.4 collective-permute-done.2
  298.5 5.4 collective-permute-done.3
  304.5 5.4 collective-permute-done.4
  310.5 5.4 collective-permute-done.5
  316.6 5.4 collective-permute-done.6
  322.6 5.4 collective-permute-done.7
  328.6 5.4 collective-permute-done.8
  334.7 5.4 collective-permute-done.9
  340.7 5.4 collective-permute-done.10
  346.8 5.4 collective-permute-done.11
  352.8 5.4 collective-permute-done.12
  358.8 5.4 collective-permute-done.13
  364.9 5.4 collective-permute-done.14
  373.4 5.5 subtract_reduce_fusion
  383.9 37.2 %psum.43 = f32[]{:T(128)} all-reduce(f32[]{:T(128)} %get-tuple-element.71), channel_id=1, replica_groups=mesh['grp'=2,'row'=16] {'grp','row'}, use_global_device_ids=true, to_apply=%region_15.16 | all-reduce | flops 1 | bytes 8 | tf_op jit(solution)/shard_map/psum | solution.py:193
  434.9 6.7 fusion.11
  448.8 15.3 %fusion.36 = bf16[4,8,64,512]{3,2,1,0:T(8,128)(2,1)} fusion(bf16[4,512,8,64]{1,3,2,0:T(8,128)(2,1)} %bitcast.233, f32[4,8,512,512]{2,3,1,0:T(8,128)} %get-tuple-element.102, f32[4,8,512]{2,1,0:T(8,128)S(1)} %get-tuple-element.101), kind=kOutput, calls=%fused_computation.80 | convolution fusion | flops 1091567616 | bytes 37814272 | tf_op jit(solution)/shard_map/shqk,sqhd->skhd/dot_general | solution.py:242
  464.1 22.7 %multiply_reduce_fusion = (f32[4,8,512]{2,1,0:T(8,128)S(1)}, f32[4,8,512,512]{2,3,1,0:T(8,128)}) fusion(f32[4,8,512,512]{2,3,1,0:T(8,128)} %get-tuple-element.102, f32[4,8,512]{2,1,0:T(8,128)S(1)} %get-tuple-element.101, bf16[4,512,8,64]{1,3,2,0:T(8,128)(2,1)} %bitcast.234, bf16[4,512,8,64]{1,3,2,0:T(8,128)(2,1)} %bitcast.231), kind=kOutput, calls=%fused_computation.8 | convolution fusion | flops 1098891264 | bytes 71434240 | tf_op jit(solution)/shard_map/sqhd,skhd->shqk/dot_general | solution.py:245
  486.8 27.6 %multiply_convert_fusion = bf16[4,8,512,512]{2,3,1,0:T(8,128)(2,1)} fusion(f32[4,8,512,512]{2,3,1,0:T(8,128)} %get-tuple-element.111, f32[4,8,512]{2,1,0:T(8,128)S(1)} %get-tuple-element.110, f32[4,8,512,512]{2,3,1,0:T(8,128)} %get-tuple-element.102, f32[4,8,512]{2,1,0:T(8,128)S(1)} %get-tuple-element.101), kind=kLoop, calls=%fused_computation.7 | loop fusion | flops 33554432 | bytes 84017152 | tf_op jit(solution)/shard_map/convert_element_type | solution.py:248
  514.4 12.9 %multiply_convert_fusion.3 = bf16[4,8,64,512]{3,2,1,0:T(8,128)(2,1)} fusion(bf16[4,512,8,64]{1,3,2,0:T(8,128)(2,1)} %bitcast.219, bf16[4,8,512,512]{2,3,1,0:T(8,128)(2,1)} %multiply_convert_fusion), kind=kOutput, calls=%fused_computation.44 | convolution fusion | flops 1075838976 | bytes 20971520 | tf_op jit(solution)/shard_map/shqk,sqhd->skhd/dot_general | solution.py:256
  527.3 10.6 %multiply_convert_fusion.4 = bf16[4,8,64,512]{3,2,1,0:T(8,128)(2,1)} fusion(bf16[4,512,8,64]{1,3,2,0:T(8,128)(2,1)} %bitcast.217, bf16[4,8,512,512]{2,3,1,0:T(8,128)(2,1)} %multiply_convert_fusion), kind=kOutput, calls=%fused_computation.45 | convolution fusion | flops 1075838976 | bytes 20971520 | tf_op jit(solution)/shard_map/shqk,skhd->sqhd/dot_general | solution.py:252
  537.9 6.5 all-to-all-start.2
  556.9 5.4 multiply_reduce_fusion.4
  569.0 6.3 fusion.26
  576.5 27.3 %scatter_custom_fusion.1 = f32[8320,256]{1,0:T(8,128)} fusion(s32[4160]{0:T(1024)} %copy-done.29, f32[64,256]{1,0:T(8,128)S(1)} %convert_reduce_fusion, f32[]{:T(128)} %constant.50.clone.1, f32[2048,256]{1,0:T(8,128)} %convert_multiply_fusion.4, f32[2048,256]{1,0:T(8,128)} %bitcast.209, f32[]{:T(128)} %constant.45.clone.1), kind=kCustom, calls=%fused_computation.36 | custom fusion | flops 2129920 | bytes 12780544 | tf_op jit(solution)/shard_map/scatter | solution.py:294
  603.8 5.3 convert_element_type.163
  609.1 6.1 all-to-all-start.3
  621.7 7.6 fusion.41
  630.2 6.0 copy.183
  637.1 62.8 %all-to-all-done.3 = bf16[16,520,256]{2,1,0:T(8,128)(2,1)} async-done(((bf16[16,520,256]{2,1,0:T(8,128)(2,1)}), bf16[16,520,256]{2,1,0:T(8,128)(2,1)}, u32[]{:S(2)}, u32[]{:S(2)}) %all-to-all-start.3) | async-done | bytes 4259872 | tf_op jit(solution)/shard_map/all_to_all | solution.py:296
  699.9 7.1 convert_select_fusion
  706.9 52.6 %scatter_custom_fusion.2 = f32[3125,256]{1,0:T(8,128)S(1)} fusion(s32[8320]{0:T(1024)S(1)} %reshape.624, f32[8320,256]{1,0:T(8,128)} %bitcast.215, f32[]{:T(128)} %constant.45.clone.1), kind=kCustom, calls=%fused_computation.83 | custom fusion | flops 2129920 | bytes 3200512 | tf_op jit(solution)/shard_map/scatter-add | solution.py:306
  762.7 77.2 %all-reduce.5.cloned.1.call-done = bf16[3125,256]{1,0:T(8,128)(2,1)} async-done(((bf16[3125,256]{1,0:T(8,128)(2,1)}), bf16[3125,256]{1,0:T(8,128)(2,1)}) %all-reduce.5.cloned.1.call-update) | async-done | bytes 1600016 | tf_op jit(solution)/shard_map/psum | solution.py:307
  844.1 39.6 %all-reduce.2 = (f32[]{:T(128)}, f32[]{:T(128)}, f32[3,256]{1,0:T(4,128)S(1)}) all-reduce(f32[]{:T(128)} %get-tuple-element.72, f32[]{:T(128)S(6)} %add.255, f32[3,256]{1,0:T(4,128)S(1)} %pad_maximum_fusion.3), channel_id=1, replica_groups=mesh['grp'=2,'row'=16] {'grp','row'}, use_global_device_ids=true, to_apply=%region_13.14 | all-reduce | flops 770 | bytes 6160 | tf_op jit(solution)/shard_map/psum | solution.py:193
  (238 shorter events, 120.7 us)
Async XLA Ops:
  7.2 9.3 %copy-start.45 = (s32[64]{0:T(128)S(1)}, s32[64]{0:T(128)}, u32[]{:S(2)}) copy-start(s32[64]{0:T(128)} %param.18) | copy-start | bytes 772
  16.7 173.2 %copy-start.29 = (s32[4160]{0:T(1024)}, s32[4160]{0:T(1024)S(1)}, u32[]{:S(2)}) copy-start(s32[4160]{0:T(1024)S(1)} %fusion.57) | copy-start | bytes 49924
  38.0 14.1 %all-to-all-start = ((s32[16,1,520]{2,1,0:T(1,128)}), s32[16,1,520]{2,1,0:T(1,128)S(1)}, u32[]{:S(2)}, u32[]{:S(2)}) async-start(s32[16,1,520]{2,1,0:T(1,128)} %all_to_all.15), calls=%async_computation | async-start | bytes 81920 | tf_op jit(solution)/shard_map/all_to_all | solution.py:129
  83.0 4.8 copy-start.22
  83.0 5.5 copy-start.47
  83.0 6.7 copy-start.46
  83.0 106.9 %copy-start.35 = (bf16[4,512]{1,0:T(4,128)(2,1)S(1)}, bf16[4,512]{1,0:T(4,128)(2,1)}, u32[]{:S(2)}) copy-start(bf16[4,512]{1,0:T(4,128)(2,1)} %param.17) | copy-start | bytes 12292
  83.0 107.0 %copy-start.36 = (f32[3,256]{1,0:T(4,128)S(1)}, f32[3,256]{1,0:T(4,128)}, u32[]{:S(2)}) copy-start(f32[3,256]{1,0:T(4,128)} %param.25) | copy-start | bytes 9220
  83.0 108.1 %all-to-all-start.1 = ((bf16[16,520,256]{2,1,0:T(8,128)(2,1)}), bf16[16,520,256]{2,1,0:T(8,128)(2,1)}, u32[]{:S(2)}, u32[]{:S(2)}) async-start(bf16[16,520,256]{2,1,0:T(8,128)(2,1)} %broadcast_select_fusion), calls=%async_computation.1 | async-start | bytes 8519680 | tf_op jit(solution)/shard_map/all_to_all | solution.py:133
  87.7 102.4 %all-gather.2.cloned.1.call-start = ((), (), s32[]{:S(2)}) async-start(), calls=%async_computation.5 | async-start | bytes 2433024 | tf_op jit(solution)/shard_map/all_gather | solution.py:111
  190.0 30.6 %copy-start.38 = (f32[1,256]{1,0:T(1,128)}, f32[1,256]{1,0:T(1,128)S(1)}, u32[]{:S(2)}) copy-start(f32[1,256]{1,0:T(1,128)S(1)} %get-tuple-element.100) | copy-start | bytes 3076
  191.0 81.1 %copy-start.10 = (f32[512,256]{1,0:T(8,128)}, f32[512,256]{1,0:T(8,128)S(1)}, u32[]{:S(2)}) copy-start(f32[512,256]{1,0:T(8,128)S(1)} %convert_bitcast_fusion) | copy-start | bytes 1572868
  203.6 17.1 %copy-start.2 = (bf16[4160,256]{1,0:T(8,128)(2,1)}, bf16[4160,256]{1,0:T(8,128)(2,1)S(1)}, u32[]{:S(2)}) copy-start(bf16[4160,256]{1,0:T(8,128)(2,1)S(1)} %gather_fusion.1) | copy-start | bytes 6389764
  205.6 18.3 %copy-start.30 = (f32[4,512]{1,0:T(4,128)}, f32[4,512]{1,0:T(4,128)S(1)}, u32[]{:S(2)}) copy-start(f32[4,512]{1,0:T(4,128)S(1)} %add.239) | copy-start | bytes 24580
  205.6 18.3 %copy-start.32 = (f32[4,512]{1,0:T(4,128)}, f32[4,512]{1,0:T(4,128)S(1)}, u32[]{:S(2)}) copy-start(f32[4,512]{1,0:T(4,128)S(1)} %rsqrt.30) | copy-start | bytes 24580
  205.6 80.1 %collective-permute-start = (bf16[64,256]{1,0:T(8,128)(2,1)S(1)}, bf16[64,256]{1,0:T(8,128)(2,1)S(1)}, u32[]{:S(2)}, u32[]{:S(2)}) collective-permute-start(bf16[64,256]{1,0:T(8,128)(2,1)S(1)} %slice.86), channel_id=1, source_target_pairs={{0,1},{1,2},{2,3},{3,4},{4,5},{5,6},{6,7},{7,8},{8,9},{9,10},{10,1... | collective-permute-start | bytes 98312 | tf_op jit(solution)/shard_map/ppermute | solution.py:34
  229.6 8.7 copy-start.16
  277.8 4.5 copy-start.17
  285.8 6.0 collective-permute-start.1
  291.8 6.0 collective-permute-start.2
  297.8 6.0 collective-permute-start.3
  303.9 6.0 collective-permute-start.4
  309.9 6.0 collective-permute-start.5
  316.0 6.0 collective-permute-start.6
  322.0 6.0 collective-permute-start.7
  328.0 6.0 collective-permute-start.8
  334.1 6.0 collective-permute-start.9
  340.1 6.0 collective-permute-start.10
  346.1 6.0 collective-permute-start.11
  352.2 6.0 collective-permute-start.12
  358.2 6.0 collective-permute-start.13
  364.3 6.0 collective-permute-start.14
  378.9 4.3 copy-start.43
  426.4 8.0 slice-start
  428.5 5.9 slice-start.1
  430.1 13.8 %copy-start.8 = (f32[2048,256]{1,0:T(8,128)}, f32[2048,256]{1,0:T(8,128)S(1)}, u32[]{:S(2)}) copy-start(f32[2048,256]{1,0:T(8,128)S(1)} %convolution_add_fusion) | copy-start | bytes 6291460
  537.9 37.5 %all-to-all-start.2 = ((bf16[16,64,256]{2,1,0:T(8,128)(2,1)}), bf16[16,64,256]{2,1,0:T(8,128)(2,1)}, u32[]{:S(2)}, u32[]{:S(2)}) async-start(bf16[16,64,256]{2,1,0:T(8,128)(2,1)} %bitcast.57), calls=%async_computation.2 | async-start | bytes 1048576 | tf_op jit(solution)/shard_map/all_to_all | solution.py:51
  556.9 5.5 copy-start.31
  556.9 5.5 copy-start.1
  609.1 90.8 %all-to-all-start.3 = ((bf16[16,520,256]{2,1,0:T(8,128)(2,1)}), bf16[16,520,256]{2,1,0:T(8,128)(2,1)}, u32[]{:S(2)}, u32[]{:S(2)}) async-start(bf16[16,520,256]{2,1,0:T(8,128)(2,1)} %bitcast.214), calls=%async_computation.3 | async-start | bytes 8519680 | tf_op jit(solution)/shard_map/all_to_all | solution.py:296
  615.2 145.7 %reduce-scatter.4.cloned.1.call-start = ((), (), s32[]{:S(2)}) async-start(), calls=%async_computation.7 | async-start | bytes 4866048
  636.2 63.7 %copy-start.28 = (pred[16,520]{1,0:T(8,128)(4,1)S(1)}, pred[16,520]{1,0:T(8,128)(4,1)}, u32[]{:S(2)}) copy-start(pred[16,520]{1,0:T(8,128)(4,1)} %copy-done.27) | copy-start | bytes 24964
  636.2 203.7 %all-reduce.5.cloned.1.call-start = ((), (), s32[]{:S(2)}) async-start(), calls=%async_computation.6 | async-start | bytes 3203072 | tf_op jit(solution)/shard_map/psum | solution.py:307
  760.9 126.1 %copy-start.37 = (f32[3,256]{1,0:T(4,128)S(1)}, f32[3,256]{1,0:T(4,128)}, u32[]{:S(2)}) copy-start(f32[3,256]{1,0:T(4,128)} %param.25) | copy-start | bytes 9220
  760.9 126.1 %copy-start.41 = (f32[3,256]{1,0:T(4,128)S(1)}, f32[3,256]{1,0:T(4,128)}, u32[]{:S(2)}) copy-start(f32[3,256]{1,0:T(4,128)} %param.26) | copy-start | bytes 9220
  760.9 126.2 %copy-start.42 = (f32[3,256]{1,0:T(4,128)S(1)}, f32[3,256]{1,0:T(4,128)}, u32[]{:S(2)}) copy-start(f32[3,256]{1,0:T(4,128)} %param.27) | copy-start | bytes 9220
  839.9 47.8 %copy-start.18 = (bf16[3125,256]{1,0:T(8,128)(2,1)S(1)}, bf16[3125,256]{1,0:T(8,128)(2,1)}, u32[]{:S(2)}) copy-start(bf16[3125,256]{1,0:T(8,128)(2,1)} %all-reduce.5.cloned.1.call-done) | copy-start | bytes 4800004
  888.2 5.5 copy-start.13
  (24 other events, 59.1 us)
Sparse Core Ops, SparseCore 0:
  92.0 97.0 all-gather.1
  636.3 114.3 reduce-scatter.3
  761.1 78.7 all-reduce.4
